TPU v7x, 256 devices: a whole 4x4x8 slice. The times are simulated.
256 devices in a mesh: row: 8 (over x, y_hi), col: 32 (over z, y_lo, core).
Axes of the slice: x: 4, y: 4 (y_hi: 2, y_lo: 2; y = y_hi * 2 + y_lo), z: 8, core: 2. Of those that a mesh axis runs over, the one named last changes fastest.
Arguments:
- grams: bfloat16 [4, 8, 32, 32, 8192], P(None, None, 'col', None, 'row'), may hold values from -2.6 to 32, as said below
- adjusted: bfloat16 [4, 8192, 1024], P(None, ('row', 'col')), may hold values from -6 to 6
Outputs:
- merged: float32 [8192, 1024], P(('row', 'col'))
- residual_norms: float32 [3], replicated
Inputs may be any that keep to these rules, and one draw needn't show every extreme that they name: `grams`: each G_m is symmetric positive definite.
All inputs are finite; a program needn't handle non-finite values.
Results may differ from a plain program's by a relative error of at most 0.0041.
Values may be sent and summed in bfloat16 or wider, within the bound.
A program may use at most 64 MiB of HBM per device.

v0:
```python
import jax
import jax.numpy as jnp
from jax import lax
from jax.sharding import Mesh
from jax.sharding import PartitionSpec as P

SWEEPS = 3
COL = ("col_0", "col_1", "col_2")
ROW = ("row_0", "row_1")
ROW_COL = ("row_0", "row_1", "col_0", "col_1", "col_2")
SHRINK = 0.9


def split_up(value, dim, peers):
    dims = value.shape
    tiles = value.reshape(*dims[:dim], peers, dims[dim] // peers, *dims[dim + 1 :])
    return jnp.moveaxis(tiles, dim, 0)


def sum_at_owner(value, axis, dim):
    tiles = split_up(value, dim, lax.axis_size(axis))
    arrived = lax.all_to_all(tiles, axis, split_axis=0, concat_axis=0, tiled=True)
    return arrived.sum(axis=0)


def one_axis_at_a_time(value, axes):
    for axis in axes:
        value = lax.psum(value, axis)
    return value


def block_solve(factor, rows):
    lower = lax.linalg.triangular_solve(factor, rows, left_side=True, lower=True)
    return lax.linalg.triangular_solve(factor, lower, left_side=True, lower=True, transpose_a=True)


def apply_gram(gram_flat, operand):
    panels = lax.all_gather(operand, COL, axis=1, tiled=True)
    partial_value = lax.slice_in_dim(gram_flat, 0, operand.shape[1] * lax.axis_size(ROW), axis=1)
    return sum_at_owner(
        jnp.einsum("ksi,kio->so", partial_value, panels, preferred_element_type=jnp.float32), ROW, 0
    )


def local(grams, adjusted):
    models = grams.shape[0]
    major = grams.shape[1]
    sub_rows = grams.shape[3]
    columns = grams.shape[4]
    here_row = lax.axis_index(ROW)
    here_col = lax.axis_index(COL)
    gram_flat = grams.reshape(models, major * sub_rows, columns)
    total32 = jnp.sum(grams.astype(jnp.float32), axis=0)
    gram_total = total32.astype(jnp.bfloat16).reshape(1, major * sub_rows, columns)
    own_rows = lax.dynamic_slice_in_dim(grams[:, :, 0], here_row, 1, 1)[:, 0]
    own_block = lax.dynamic_slice_in_dim(own_rows, here_col * sub_rows, sub_rows, 2).astype(
        jnp.float32
    )
    diag_each = jnp.diagonal(own_block, axis1=1, axis2=2)
    diag_sum = jnp.sum(diag_each, 0)
    precond = SHRINK * jnp.sum(own_block, 0) + (1.0 - SHRINK) * jnp.diag(diag_sum)
    factor = jnp.linalg.cholesky(precond)
    weights32 = adjusted.astype(jnp.float32)
    rhs = SHRINK * apply_gram(gram_flat, adjusted)
    rhs = rhs + (1.0 - SHRINK) * jnp.sum(diag_each[:, :, None] * weights32, 0)
    rhs_local = jnp.sum(rhs * rhs)
    merged = jnp.mean(weights32, 0)
    squares_list = []
    for sweep_index in range(SWEEPS):
        image = SHRINK * apply_gram(gram_total, merged.astype(jnp.bfloat16)[None])
        image = image + (1.0 - SHRINK) * diag_sum[:, None] * merged
        resid = rhs - image
        squares_local = jnp.sum(resid * resid)
        squares_list.append(squares_local)
        merged = merged + block_solve(factor, resid)
    totals = one_axis_at_a_time(jnp.stack(squares_list + [rhs_local]), ROW_COL)
    norms = jnp.sqrt(totals[:SWEEPS] / totals[SWEEPS])
    return (merged, norms)


def solution(mesh):
    finer = Mesh(mesh.devices.reshape(4, 2, 8, 2, 2), ("row_0", "row_1", "col_0", "col_1", "col_2"))
    placed = (P(None, None, COL, None, ROW), P(None, ROW_COL, None))
    return jax.shard_map(
        local, mesh=finer, in_specs=placed, out_specs=(P(ROW_COL, None), P()), check_vma=False
    )
```

profile of v0, /device:TPU:1, one launch (start us, length us, event | category | flops | bytes accessed | tf_op | source)
XLA Modules:
  0.0 421.2 jit_solution(12293854520328392393)
XLA Ops:
  7.3 1.5 copy-done
  13.0 67.6 %all-gather.10.cloned.1.call-done = bf16[1024,1024]{1,0:T(8,128)(2,1)} async-done(((bf16[32,1024]{1,0:T(8,128)(2,1)}), bf16[1024,1024]{1,0:T(8,128)(2,1)}) %all-gather.10.cloned.1.call-update) | async-done | bytes 2097168 | tf_op jit(solution)/shard_map/all_gather | solution.py:38
  80.5 3.3 fusion.7
  83.8 6.1 %all-to-all-start.1 = ((f32[8,32,1024]{2,1,0:T(8,128)}), f32[8,32,1024]{2,1,0:T(8,128)}, u32[]{:S(2)}, u32[]{:S(2)}) async-start(f32[8,32,1024]{2,1,0:T(8,128)} %fusion.7), calls=%async_computation.1 | async-start | bytes 2097152 | tf_op jit(solution)/shard_map/all_to_all | solution.py:22
  90.2 67.5 %all-gather.8.cloned.1.call-done = bf16[4,1024,1024]{2,1,0:T(8,128)(2,1)} async-done(((bf16[4,32,1024]{2,1,0:T(8,128)(2,1)}), bf16[4,1024,1024]{2,1,0:T(8,128)(2,1)}) %all-gather.8.cloned.1.call-update) | async-done | bytes 8388624 | tf_op jit(solution)/shard_map/all_gather | solution.py:38
  157.7 6.7 %fusion.9 = f32[8,32,1024]{2,1,0:T(8,128)} fusion(bf16[4,1024,1024]{2,1,0:T(8,128)(2,1)} %all-gather.8.cloned.1.call-done, bf16[4,8,1,32,1024]{4,3,2,1,0:T(8,128)(2,1)S(1)} %copy-done), kind=kOutput, calls=%fused_computation.10 | convolution fusion | flops 2147483648 | bytes 11534336 | tf_op jit(solution)/shard_map/ksi,kio->so/dot_general | solution.py:41
  164.4 7.1 %all-to-all-start = ((f32[8,32,1024]{2,1,0:T(8,128)}), f32[8,32,1024]{2,1,0:T(8,128)}, u32[]{:S(2)}, u32[]{:S(2)}) async-start(f32[8,32,1024]{2,1,0:T(8,128)} %fusion.9), calls=%async_computation | async-start | bytes 2097152 | tf_op jit(solution)/shard_map/all_to_all | solution.py:22
  171.8 2.9 cholesky.19
  176.1 2.4 custom-call.16
  178.5 1.3 reduce_sum.126
  179.9 7.6 %all-to-all-done = f32[8,32,1024]{2,1,0:T(8,128)} async-done(((f32[8,32,1024]{2,1,0:T(8,128)}), f32[8,32,1024]{2,1,0:T(8,128)}, u32[]{:S(2)}, u32[]{:S(2)}) %all-to-all-start) | async-done | bytes 1048608 | tf_op jit(solution)/shard_map/all_to_all | solution.py:22
  190.8 62.2 %all-gather.12.cloned.1.call-done = bf16[1024,1024]{1,0:T(8,128)(2,1)} async-done(((bf16[32,1024]{1,0:T(8,128)(2,1)}), bf16[1024,1024]{1,0:T(8,128)(2,1)}) %all-gather.12.cloned.1.call-update) | async-done | bytes 2097168 | tf_op jit(solution)/shard_map/all_gather | solution.py:38
  253.0 2.3 fusion.5
  255.3 21.7 %all_to_all.20 = f32[8,32,1024]{2,1,0:T(8,128)} all-to-all(f32[8,32,1024]{2,1,0:T(8,128)S(1)} %fusion.5), channel_id=1, replica_groups=mesh['row_0'=4,'row_1'=2,'col_0'=8,'col_1'=2,'col_2'=2] {'row_0','row_1'}, dimensions={0} | all-to-all | bytes 2097152 | tf_op jit(solution)/shard_map/all_to_all | solution.py:22
  280.2 62.7 %all-gather.14.cloned.1.call-done = bf16[1024,1024]{1,0:T(8,128)(2,1)} async-done(((bf16[32,1024]{1,0:T(8,128)(2,1)}), bf16[1024,1024]{1,0:T(8,128)(2,1)}) %all-gather.14.cloned.1.call-update) | async-done | bytes 2097168 | tf_op jit(solution)/shard_map/all_gather | solution.py:38
  342.9 2.3 fusion.3
  345.2 21.6 %all_to_all.21 = f32[8,32,1024]{2,1,0:T(8,128)S(1)} all-to-all(f32[8,32,1024]{2,1,0:T(8,128)S(1)} %fusion.3), channel_id=1, replica_groups=mesh['row_0'=4,'row_1'=2,'col_0'=8,'col_1'=2,'col_2'=2] {'row_0','row_1'}, dimensions={0} | all-to-all | bytes 2097152 | tf_op jit(solution)/shard_map/all_to_all | solution.py:22
  366.9 1.4 multiply_reduce_fusion.1
  368.3 2.7 pad_maximum_fusion
  371.0 6.9 %psum.35 = f32[4]{0:T(128)S(1)} all-reduce(f32[4]{0:T(128)S(1)} %pad_maximum_fusion), channel_id=1, replica_groups=mesh['row_0'=4,'row_1'=2,'col_0'=8,'col_1'=2,'col_2'=2] {'row_0'}, use_global_device_ids=true, to_apply=%region_15.18 | all-reduce | flops 4 | bytes 32 | tf_op jit(solution)/shard_map/psum | solution.py:28
  377.9 5.3 %psum.36 = f32[4]{0:T(128)S(1)} all-reduce(f32[4]{0:T(128)S(1)} %psum.35), channel_id=1, replica_groups=mesh['row_0'=4,'row_1'=2,'col_0'=8,'col_1'=2,'col_2'=2] {'row_1'}, use_global_device_ids=true, to_apply=%region_16.19 | all-reduce | flops 4 | bytes 32 | tf_op jit(solution)/shard_map/psum | solution.py:28
  383.1 12.5 %psum.37 = f32[4]{0:T(128)S(1)} all-reduce(f32[4]{0:T(128)S(1)} %psum.36), channel_id=1, replica_groups=mesh['row_0'=4,'row_1'=2,'col_0'=8,'col_1'=2,'col_2'=2] {'col_0'}, use_global_device_ids=true, to_apply=%region_17.20 | all-reduce | flops 4 | bytes 32 | tf_op jit(solution)/shard_map/psum | solution.py:28
  396.0 4.1 psum.38
  401.0 11.8 %psum.39 = f32[4]{0:T(128)S(1)} all-reduce(f32[4]{0:T(128)S(1)} %psum.38), channel_id=1, replica_groups=mesh['row_0'=4,'row_1'=2,'col_0'=8,'col_1'=2,'col_2'=2] {'col_2'}, use_global_device_ids=true, to_apply=%region_19.22 | all-reduce | flops 4 | bytes 32 | tf_op jit(solution)/shard_map/psum | solution.py:28
  (44 shorter events, 15.8 us)
Async XLA Ops:
  7.2 1.6 copy-start
  7.2 73.4 %all-gather.10.cloned.1.call-start = ((), (), s32[]{:S(2)}) async-start(), calls=%async_computation.5 | async-start | bytes 2162688 | tf_op jit(solution)/shard_map/all_gather | solution.py:38
  11.8 146.0 %all-gather.8.cloned.1.call-start = ((), (), s32[]{:S(2)}) async-start(), calls=%async_computation.4 | async-start | bytes 8650752 | tf_op jit(solution)/shard_map/all_gather | solution.py:38
  83.8 80.6 %all-to-all-start.1 = ((f32[8,32,1024]{2,1,0:T(8,128)}), f32[8,32,1024]{2,1,0:T(8,128)}, u32[]{:S(2)}, u32[]{:S(2)}) async-start(f32[8,32,1024]{2,1,0:T(8,128)} %fusion.7), calls=%async_computation.1 | async-start | bytes 2097152 | tf_op jit(solution)/shard_map/all_to_all | solution.py:22
  164.4 23.0 %all-to-all-start = ((f32[8,32,1024]{2,1,0:T(8,128)}), f32[8,32,1024]{2,1,0:T(8,128)}, u32[]{:S(2)}, u32[]{:S(2)}) async-start(f32[8,32,1024]{2,1,0:T(8,128)} %fusion.9), calls=%async_computation | async-start | bytes 2097152 | tf_op jit(solution)/shard_map/all_to_all | solution.py:22
  171.5 81.4 %all-gather.12.cloned.1.call-start = ((), (), s32[]{:S(2)}) async-start(), calls=%async_computation.6 | async-start | bytes 2162688 | tf_op jit(solution)/shard_map/all_gather | solution.py:38
  178.5 99.7 %copy-start.1 = (f32[32]{0:T(128)}, f32[32]{0:T(128)S(1)}, u32[]{:S(2)}) copy-start(f32[32]{0:T(128)S(1)} %get-tuple-element.14) | copy-start | bytes 388
  190.7 152.2 %all-gather.14.cloned.1.call-start = ((), (), s32[]{:S(2)}) async-start(), calls=%async_computation.7 | async-start | bytes 2162688 | tf_op jit(solution)/shard_map/all_gather | solution.py:38
Sparse Core Ops, SparseCore 0:
  11.9 68.5 all-gather.9
  82.4 75.3 all-gather.7
  190.8 62.0 all-gather.11
  280.4 62.5 all-gather.13
where the time goes:
time: 422 us; the launch traced here: 421 us
  waiting for transfers between devices  268 us (64%)
  blocking collectives  83.9 us (20%)
  other arithmetic  20 us (5%)
  matrix products  18.2 us (4%)
  between operations  13.9 us (3%)
  starting transfers between devices  13.4 us (3%)
    all_gather x4, waiting for transfers between devices, apply_gram(): panels = lax.all_gather(operand, COL, axis=1, tiled=True)  260 us
    all_to_all x2, blocking collectives, sum_at_owner(): lax.all_to_all(tiles, axis, split_axis=0, concat_axis=0, tiled=True)  43.3 us
    psum x5, blocking collectives, one_axis_at_a_time(): value = lax.psum(value, axis)  40.5 us
    dot_general x4, matrix products, apply_gram(): jnp.einsum('ksi,kio->so', partial_value, panels, preferred_element_type=j...  14.5 us
    all_to_all x2, starting transfers between devices, sum_at_owner(): lax.all_to_all(tiles, axis, split_axis=0, concat_axis=0, tiled=True)  13.2 us
  transfers between devices with their start and end apart: 6, of which 5 were waited for; matrix products, arithmetic and copies ran while one was open for 4% of the time, Pallas kernels for 0%

commit v1 on v0

--- a/solution.py
+++ b/solution.py
@@ -35,7 +35,9 @@
 
 
 def apply_gram(gram_flat, operand):
-    panels = lax.all_gather(operand, COL, axis=1, tiled=True)
+    panels = jnp.concatenate(
+        lax.all_to_all(jnp.stack([operand] * lax.axis_size(COL)), COL, 0, 0), axis=1
+    )
     partial_value = lax.slice_in_dim(gram_flat, 0, operand.shape[1] * lax.axis_size(ROW), axis=1)
     return sum_at_owner(
         jnp.einsum("ksi,kio->so", partial_value, panels, preferred_element_type=jnp.float32), ROW, 0

time: 422 us -> 510 us (1.21)
  blocking collectives: 83.9 us -> 249 us
  waiting for transfers between devices: 268 us -> 191 us
  local copies, waits for them, and re-layouts: 3.51 us -> 17.1 us
  between operations: 13.9 us -> 0.84 us
    all_gather x4 -> x0, waiting for transfers between devices: 260 us -> none  [apply_gram(): panels = lax.all_gather(operand, COL, axis=1, tiled=True)]
    all_to_all x0 -> x1, waiting for transfers between devices: none -> 183 us  [apply_gram(): lax.all_to_all(jnp.stack([operand] * lax.axis_size(COL)), COL, 0, 0)]
    all_to_all x0 -> x3, blocking collectives: none -> 173 us  [apply_gram(): lax.all_to_all(jnp.stack([operand] * lax.axis_size(COL)), COL, 0, 0)]
    reshape x0 -> x1, local copies, waits for them, and re-layouts: none -> 8.47 us  [apply_gram(): jnp.concatenate(lax.all_to_all(jnp.stack([operand] * lax.axis_size(COL)),...]
    all_to_all x2, blocking collectives: 43.3 us -> 36.9 us  [sum_at_owner(): lax.all_to_all(tiles, axis, split_axis=0, concat_axis=0, tiled=True)]
    all_to_all x0 -> x1, starting transfers between devices: none -> 5.29 us  [apply_gram(): lax.all_to_all(jnp.stack([operand] * lax.axis_size(COL)), COL, 0, 0)]
  transfers between devices with their start and end apart: 6 -> 3, of which waited for: 5 -> 3; matrix products, arithmetic and copies ran while one was open for 4% -> 5% of each run, Pallas kernels for 0% -> 0%
where the time goes in v1:
time: 510 us; the launch traced here: 509 us
  blocking collectives  249 us (49%)
  waiting for transfers between devices  191 us (37%)
  other arithmetic  19.4 us (4%)
  starting transfers between devices  18 us (4%)
  local copies, waits for them, and re-layouts  17.1 us (3%)
  matrix products  13.8 us (3%)
    all_to_all x1, waiting for transfers between devices, apply_gram(): lax.all_to_all(jnp.stack([operand] * lax.axis_size(COL)), COL, 0, 0)  183 us
    all_to_all x3, blocking collectives, apply_gram(): lax.all_to_all(jnp.stack([operand] * lax.axis_size(COL)), COL, 0, 0)  173 us
    psum x5, blocking collectives, one_axis_at_a_time(): value = lax.psum(value, axis)  39.2 us
    all_to_all x2, blocking collectives, sum_at_owner(): lax.all_to_all(tiles, axis, split_axis=0, concat_axis=0, tiled=True)  36.9 us
    all_to_all x2, starting transfers between devices, sum_at_owner(): lax.all_to_all(tiles, axis, split_axis=0, concat_axis=0, tiled=True)  12.7 us
    dot_general x4, matrix products, apply_gram(): jnp.einsum('ksi,kio->so', partial_value, panels, preferred_element_type=j...  11.4 us
  transfers between devices with their start and end apart: 3, of which 3 were waited for; matrix products, arithmetic and copies ran while one was open for 5% of the time, Pallas kernels for 0%

profile of v1, /device:TPU:1, one launch (start us, length us, event | category | flops | bytes accessed | tf_op | source)
XLA Modules:
  0.0 508.7 jit_solution(4402069886753916995)
XLA Ops:
  0.7 1.5 copy-done
  4.9 61.7 %all_to_all.40 = bf16[32,1,32,1024]{3,2,1,0:T(8,128)(2,1)} all-to-all(bf16[32,1,32,1024]{3,2,1,0:T(8,128)(2,1)S(1)} %stack.19), channel_id=1, replica_groups=mesh['row_0'=4,'row_1'=2,'col_0'=8,'col_1'=2,'col_2'=2] {'col_0','col_1'..., dimensions={0} | all-to-all | bytes 4194304 | tf_op jit(solution)/shard_map/all_to_all | solution.py:39
  66.6 4.3 stack.18
  70.8 5.3 %all-to-all-start = ((bf16[32,4,32,1024]{3,2,1,0:T(8,128)(2,1)}), bf16[32,4,32,1024]{3,2,1,0:T(8,128)(2,1)}, u32[]{:S(2)}, u32[]{:S(2)}) async-start(bf16[32,4,32,1024]{3,2,1,0:T(8,128)(2,1)} %stack.18), calls=%async_computation | async-start | bytes 16777216 | tf_op jit(solution)/shard_map/all_to_all | solution.py:39
  76.6 3.3 fusion.20
  79.9 182.8 %all-to-all-done = bf16[32,4,32,1024]{3,2,1,0:T(8,128)(2,1)} async-done(((bf16[32,4,32,1024]{3,2,1,0:T(8,128)(2,1)}), bf16[32,4,32,1024]{3,2,1,0:T(8,128)(2,1)}, u32[]{:S(2)}, u32[]{:S(2)}) %all-to-all-start) | async-done | bytes 8388640 | tf_op jit(solution)/shard_map/all_to_all | solution.py:39
  262.7 6.4 %all-to-all-start.3 = ((f32[8,32,1024]{2,1,0:T(8,128)}), f32[8,32,1024]{2,1,0:T(8,128)}, u32[]{:S(2)}, u32[]{:S(2)}) async-start(f32[8,32,1024]{2,1,0:T(8,128)} %fusion.20), calls=%async_computation.3 | async-start | bytes 2097152 | tf_op jit(solution)/shard_map/all_to_all | solution.py:22
  269.4 8.5 %copy.14 = bf16[4,32,32,1024]{3,2,1,0:T(8,128)(2,1)} copy(bf16[4,32,32,1024]{3,2,0,1:T(8,128)(2,1)} %bitcast.10) | data formatting | bytes 16777216 | tf_op jit(solution)/shard_map/reshape | solution.py:38
  277.8 6.7 %fusion.2 = f32[8,32,1024]{2,1,0:T(8,128)} fusion(bf16[4,1024,1024,1]{2,1,3,0:T(8,128)(2,1)} %bitcast.87, bf16[4,8,1,32,1024]{4,3,2,1,0:T(8,128)(2,1)S(1)} %copy-done), kind=kOutput, calls=%fused_computation.3 | convolution fusion | flops 2147483648 | bytes 11534336 | tf_op jit(solution)/shard_map/ksi,kio->so/dot_general | solution.py:43
  284.9 6.3 %all-to-all-start.1 = ((f32[8,32,1024]{2,1,0:T(8,128)}), f32[8,32,1024]{2,1,0:T(8,128)}, u32[]{:S(2)}, u32[]{:S(2)}) async-start(f32[8,32,1024]{2,1,0:T(8,128)} %fusion.2), calls=%async_computation.1 | async-start | bytes 2097152 | tf_op jit(solution)/shard_map/all_to_all | solution.py:22
  291.5 2.9 cholesky.19
  295.8 2.4 custom-call.16
  299.5 7.5 %all-to-all-done.1 = f32[8,32,1024]{2,1,0:T(8,128)} async-done(((f32[8,32,1024]{2,1,0:T(8,128)}), f32[8,32,1024]{2,1,0:T(8,128)}, u32[]{:S(2)}, u32[]{:S(2)}) %all-to-all-start.1) | async-done | bytes 1048608 | tf_op jit(solution)/shard_map/all_to_all | solution.py:22
  309.8 54.2 %all_to_all.41 = bf16[32,1,32,1024]{3,2,1,0:T(8,128)(2,1)S(1)} all-to-all(bf16[32,1,32,1024]{3,2,1,0:T(8,128)(2,1)S(1)} %stack.20), channel_id=1, replica_groups=mesh['row_0'=4,'row_1'=2,'col_0'=8,'col_1'=2,'col_2'=2] {'col_0','col_1'..., dimensions={0} | all-to-all | bytes 4194304 | tf_op jit(solution)/shard_map/all_to_all | solution.py:39
  364.8 18.7 %all_to_all.42 = f32[8,32,1024]{2,1,0:T(8,128)} all-to-all(f32[8,32,1024]{2,1,0:T(8,128)S(1)} %fusion.21), channel_id=1, replica_groups=mesh['row_0'=4,'row_1'=2,'col_0'=8,'col_1'=2,'col_2'=2] {'row_0','row_1'}, dimensions={0} | all-to-all | bytes 2097152 | tf_op jit(solution)/shard_map/all_to_all | solution.py:22
  386.3 57.0 %all_to_all.43 = bf16[32,1,32,1024]{3,2,1,0:T(8,128)(2,1)S(1)} all-to-all(bf16[32,1,32,1024]{3,2,1,0:T(8,128)(2,1)S(1)} %stack.21), channel_id=1, replica_groups=mesh['row_0'=4,'row_1'=2,'col_0'=8,'col_1'=2,'col_2'=2] {'col_0','col_1'..., dimensions={0} | all-to-all | bytes 4194304 | tf_op jit(solution)/shard_map/all_to_all | solution.py:39
  444.1 18.2 %all_to_all.44 = f32[8,32,1024]{2,1,0:T(8,128)S(1)} all-to-all(f32[8,32,1024]{2,1,0:T(8,128)S(1)} %fusion.22), channel_id=1, replica_groups=mesh['row_0'=4,'row_1'=2,'col_0'=8,'col_1'=2,'col_2'=2] {'row_0','row_1'}, dimensions={0} | all-to-all | bytes 2097152 | tf_op jit(solution)/shard_map/all_to_all | solution.py:22
  462.3 1.5 multiply_reduce_fusion.1
  463.8 2.6 pad_maximum_fusion
  466.4 6.9 %psum.35 = f32[4]{0:T(128)S(1)} all-reduce(f32[4]{0:T(128)S(1)} %pad_maximum_fusion), channel_id=1, replica_groups=mesh['row_0'=4,'row_1'=2,'col_0'=8,'col_1'=2,'col_2'=2] {'row_0'}, use_global_device_ids=true, to_apply=%region_15.18 | all-reduce | flops 4 | bytes 32 | tf_op jit(solution)/shard_map/psum | solution.py:28
  473.4 5.3 %psum.36 = f32[4]{0:T(128)S(1)} all-reduce(f32[4]{0:T(128)S(1)} %psum.35), channel_id=1, replica_groups=mesh['row_0'=4,'row_1'=2,'col_0'=8,'col_1'=2,'col_2'=2] {'row_1'}, use_global_device_ids=true, to_apply=%region_16.19 | all-reduce | flops 4 | bytes 32 | tf_op jit(solution)/shard_map/psum | solution.py:28
  478.6 10.7 %psum.37 = f32[4]{0:T(128)S(1)} all-reduce(f32[4]{0:T(128)S(1)} %psum.36), channel_id=1, replica_groups=mesh['row_0'=4,'row_1'=2,'col_0'=8,'col_1'=2,'col_2'=2] {'col_0'}, use_global_device_ids=true, to_apply=%region_17.20 | all-reduce | flops 4 | bytes 32 | tf_op jit(solution)/shard_map/psum | solution.py:28
  489.6 4.4 psum.38
  494.9 11.9 %psum.39 = f32[4]{0:T(128)S(1)} all-reduce(f32[4]{0:T(128)S(1)} %psum.38), channel_id=1, replica_groups=mesh['row_0'=4,'row_1'=2,'col_0'=8,'col_1'=2,'col_2'=2] {'col_2'}, use_global_device_ids=true, to_apply=%region_19.22 | all-reduce | flops 4 | bytes 32 | tf_op jit(solution)/shard_map/psum | solution.py:28
  (44 shorter events, 16.8 us)
Async XLA Ops:
  0.6 1.6 copy-start
  4.9 61.7 %copy-start.1 = (bf16[4,32,1024]{2,1,0:T(8,128)(2,1)S(1)}, bf16[4,32,1024]{2,1,0:T(8,128)(2,1)}, u32[]{:S(2)}) copy-start(bf16[4,32,1024]{2,1,0:T(8,128)(2,1)} %param.7) | copy-start | bytes 786436
  70.8 191.9 %all-to-all-start = ((bf16[32,4,32,1024]{3,2,1,0:T(8,128)(2,1)}), bf16[32,4,32,1024]{3,2,1,0:T(8,128)(2,1)}, u32[]{:S(2)}, u32[]{:S(2)}) async-start(bf16[32,4,32,1024]{3,2,1,0:T(8,128)(2,1)} %stack.18), calls=%async_computation | async-start | bytes 16777216 | tf_op jit(solution)/shard_map/all_to_all | solution.py:39
  262.7 22.2 %all-to-all-start.3 = ((f32[8,32,1024]{2,1,0:T(8,128)}), f32[8,32,1024]{2,1,0:T(8,128)}, u32[]{:S(2)}, u32[]{:S(2)}) async-start(f32[8,32,1024]{2,1,0:T(8,128)} %fusion.20), calls=%async_computation.3 | async-start | bytes 2097152 | tf_op jit(solution)/shard_map/all_to_all | solution.py:22
  284.9 22.1 %all-to-all-start.1 = ((f32[8,32,1024]{2,1,0:T(8,128)}), f32[8,32,1024]{2,1,0:T(8,128)}, u32[]{:S(2)}, u32[]{:S(2)}) async-start(f32[8,32,1024]{2,1,0:T(8,128)} %fusion.2), calls=%async_computation.1 | async-start | bytes 2097152 | tf_op jit(solution)/shard_map/all_to_all | solution.py:22
  298.2 86.6 %copy-start.2 = (f32[32]{0:T(128)}, f32[32]{0:T(128)S(1)}, u32[]{:S(2)}) copy-start(f32[32]{0:T(128)S(1)} %get-tuple-element.14) | copy-start | bytes 388
